TPU v7x, 128 devices: a whole 4x4x4 slice. The times are simulated.
128 devices in a mesh: tp: 4 (over z), dp: 4 (over y), pp: 8 (over x, core).
Axes of the slice: x: 4, y: 4, z: 4, core: 2. Of those that a mesh axis runs over, the one named last changes fastest.
Arguments:
- master: float32 [50304, 768], P('tp')
- exp_avg: float32 [50304, 768], P('tp')
- exp_avg_sq: float32 [50304, 768], P('tp')
- stage_ids: int32 [8, 24, 384], P('pp', 'dp')
- stage_acts: bfloat16 [8, 24, 384, 768], P('pp', 'dp')
Outputs:
- output 1: float32 [50304, 768], P('tp')
- output 2: float32 [50304, 768], P('tp')
- output 3: float32 [50304, 768], P('tp')
- output 4: bfloat16 [50304, 768], P('tp')
All inputs are finite; a program needn't handle non-finite values.
Results may differ from a plain program's by a relative error of at most 0.001.
Values sent between devices are 32-bit elements.
A program may use at most 1 GiB of HBM per device.

v0:
```python
import functools

import jax
import jax.numpy as jnp
from jax import lax
from jax.experimental import pallas as pl
from jax.experimental.pallas import tpu as pltpu
from jax.sharding import PartitionSpec as P


LEARN_RATE = 0.003
BETA_ONE = 0.9
BETA_TWO = 0.95
ADAM_EPS = 1e-8
WEIGHT_DECAY = 0.1
CLIP_NORM = 1.0
OPT_STEP = 10


MESH = pl.DeviceIdType.MESH
ANY = pl.BlockSpec(memory_space=pl.ANY)
VMEM = pl.BlockSpec(memory_space=pltpu.VMEM)
NEG_BIG = float("-inf")


def in_block(local, block_rows):
    return jnp.where(local < block_rows, local, -(2**30))


def remote(src, dst, send_sem, recv_sem, device):
    return pltpu.make_async_remote_copy(
        src_ref=src, dst_ref=dst, send_sem=send_sem, recv_sem=recv_sem, device_id=device, device_id_type=MESH
    )


LANE = 128
PIECE_TOK = 64


def front_kernel(
    cfg, master, acts, toks, *refs
):
    n_tp, n_dp, n_pp, chunks, bases, piece, block_rows = cfg
    group_outs, factor_out = refs[:4], refs[4]
    (h_f, x_f, h_bf, x_bf, part, e_bf, logit, dlog, lse, lse_a, lse_b, rs_a, rs_b, lab, ids, sq, sq_all, fac) = refs[5:23]
    (e_sem, load_sem, tok_send, tok_recv, st_recv, d2d_send, x_send, z_send, lse_send, lse_recv, rs_send, rs_recv, sq_send, sq_recv, out_sem) = refs[23:38]
    (f_send, f_recv, p_send, p_recv, ready) = refs[38:]
    me = lax.axis_index("pp")
    tpi = lax.axis_index("tp")
    dpi = lax.axis_index("dp")
    n_x = n_pp // 2
    x, core = me // 2, lax.rem(me, 2)
    n_chunk = len(chunks)
    rows_chunk = n_dp * piece
    tok_count, dim = h_f.shape
    half_tok = tok_count // 2
    tiles_a = (half_tok // LANE + 1) // 2
    tiles_b = half_tok // LANE - tiles_a
    per_tile = LANE // PIECE_TOK
    counts = (tiles_a * per_tile, tiles_b * per_tile) * 2
    tok_a = tiles_a * LANE

    def row_at(c, d, x_at, core_at):
        color, s, count = chunks[c]
        owner = d * n_pp + x_at * 2 + core_at if color == 0 else x_at * (2 * n_dp) + d * 2 + core_at
        return bases[color] + (owner * count + s) * piece

    def first_row(c, d):
        return row_at(c, d, x, core)

    def whole(c, d):
        return row_at(c, d, n_x - 1, 1) + piece <= block_rows

    tail = block_rows % piece

    def row_copy(c, d, n):
        slot = c * rows_chunk + d * piece
        start = pl.multiple_of(first_row(c, d), 8)
        return pltpu.make_async_copy(master.at[pl.ds(start, n), :], part.at[pl.ds(slot, n), :], e_sem.at[c])

    def on_rows(act):
        for c in range(n_chunk):
            for d in range(n_dp):
                if whole(c, d):
                    act(row_copy(c, d, piece))
                else:

                    @pl.when(first_row(c, d) + piece <= block_rows)
                    def _(c=c, d=d):
                        act(row_copy(c, d, piece))

                    if tail:

                        @pl.when(first_row(c, d) + tail == block_rows)
                        def _(c=c, d=d):
                            act(row_copy(c, d, tail))

    src_h = me == n_pp - 1
    src_x = me == 0

    def source_loads(buf, tok):
        return (pltpu.make_async_copy(acts, buf, load_sem.at[0]), pltpu.make_async_copy(toks, tok, load_sem.at[1]))

    for is_src, buf, tok in ((src_h, h_bf, lab), (src_x, x_bf, ids)):

        @pl.when(is_src)
        def _(buf=buf, tok=tok):
            for c in source_loads(buf, tok):
                c.start()

    on_rows(lambda c: c.start())
    barrier = pltpu.get_barrier_semaphore()
    for axis, idx, size in (("pp", me, n_pp), ("tp", tpi, n_tp), ("dp", dpi, n_dp)):
        for k in range(1, size):
            pl.semaphore_signal(barrier, inc=1, device_id={axis: lax.rem(idx + k, size)}, device_id_type=MESH)

    for is_src, buf, tok, wide in ((src_h, h_bf, lab, h_f), (src_x, x_bf, ids, x_f)):

        @pl.when(is_src)
        def _(buf=buf, tok=tok, wide=wide):
            for c in source_loads(buf, tok):
                c.wait()

            def widen(t, _):
                at = pl.ds(pl.multiple_of(t * LANE, LANE), LANE)
                wide[at, :] = buf[at, :].astype(jnp.float32)
                return 0

            lax.fori_loop(0, tok_count // LANE, widen, 0)

    pl.semaphore_wait(barrier, n_pp + n_tp + n_dp - 3)

    def tok_copy(which, ref, k):
        return remote(ref, ref, tok_send.at[which, k], tok_recv.at[which], {"pp": lax.rem(me + k, n_pp)})

    for which, is_src, tok in ((0, src_h, lab), (1, src_x, ids)):

        @pl.when(is_src)
        def _(which=which, tok=tok):
            for k in range(1, n_pp):
                tok_copy(which, tok, k).start()

    half = lax.rem(tpi, 2)
    partner = {"pp": x * 2 + 1 - core}
    right = {"pp": lax.rem(x + 1, n_x) * 2 + core}
    left = {"pp": lax.rem(x + n_x - 1, n_x) * 2 + core}
    z_up = {"tp": lax.rem(tpi + 1, n_tp)}
    z_down = {"tp": lax.rem(tpi + n_tp - 1, n_tp)}
    hop = 2 * per_tile // 2
    lag = (hop * (n_x - 2) + hop) // per_tile + 1

    def stream(s, buf):
        handler = core == 1 - s
        u = lax.rem(x - (n_x - 1, 0)[s] + n_x, n_x)
        base = [half * half_tok, half * half_tok + tok_a, (1 - half) * half_tok, (1 - half) * half_tok + tok_a]
        ahead = jnp.maximum(u - 1, 0) * hop
        behind = jnp.where(u == 0, 0, (n_x - 1 - u) * hop)
        second = jnp.where(u == 0, 0, hop)
        offs = (ahead, behind, ahead + second, behind + second)

        def rows(kind, p, n):
            return buf.at[pl.ds(pl.multiple_of(base[kind] + p * PIECE_TOK, PIECE_TOK), n), :]

        def copy(kind, p, to, sem, device, n=PIECE_TOK):
            at = rows(kind, p, n)
            return remote(at, at, sem, st_recv.at[s, to, p], device)

        def outs(kind):
            found = [(handler, kind, d2d_send.at[s, kind], partner)]
            if kind == 0:
                found.append((handler & (u <= n_x - 2), 0, x_send.at[s, 0], right))
                found.append((handler & (u > 0), 2, z_send.at[s, 0], z_up))
            if kind == 1:
                found.append((handler & ((u == 0) | (u >= 2)), 1, x_send.at[s, 1], left))
                found.append((handler & (u > 0), 3, z_send.at[s, 1], z_down))
            return found

        def slot(t):
            for kind in range(4):
                p = t - offs[kind]

                @pl.when((p >= 0) & (p < counts[kind]))
                def _(kind=kind, p=p):
                    @pl.when(jnp.logical_not(handler & (u == 0)))
                    def _():
                        copy(kind, p, kind, d2d_send.at[s, kind], partner).wait_recv()

                    for cond, to, sem, device in reversed(outs(kind)):

                        @pl.when(cond)
                        def _(to=to, sem=sem, device=device):
                            copy(kind, p, to, sem, device).start()

        def drain():
            for kind in range(4):
                for cond, to, sem, device in outs(kind):

                    @pl.when(cond)
                    def _(kind=kind, to=to, sem=sem, device=device):
                        copy(kind, 0, to, sem, device, counts[kind] * PIECE_TOK).wait_send()

        return slot, drain

    h_slot, h_drain = stream(0, h_f)
    x_slot, x_drain = stream(1, x_f)
    n_it = lag + tiles_b
    x_first = tiles_a

    def x_it(it):
        for k in range(per_tile):
            x_slot(it * per_tile + k)

    def prepare_rows():
        on_rows(lambda c: c.wait())
        for c in range(n_chunk):
            for d in range(n_dp):
                at = pl.ds(c * rows_chunk + d * piece, piece)
                rows = part[at, :]
                if not whole(c, d):
                    inside = lax.broadcasted_iota(jnp.int32, (piece, dim), 0) + first_row(c, d) < block_rows
                    rows = jnp.where(inside, rows, 0.0)
                e_bf[at, :] = rows.astype(jnp.bfloat16)

    wide_tile = 2 * LANE

    def logit_pair(t_one, t_two):
        ats = [pl.ds(pl.multiple_of(t, LANE), LANE) for t in (t_one, t_two)]
        h_tile = jnp.concatenate([h_f[at, :].astype(jnp.bfloat16) for at in ats], axis=0)
        for i, at in enumerate(ats):
            h_bf[at, :] = h_tile[i * LANE : (i + 1) * LANE]
        top = jnp.full((8, wide_tile), NEG_BIG, jnp.float32)
        iota_p = lax.broadcasted_iota(jnp.int32, (piece, wide_tile), 0)
        for c in range(n_chunk):
            rows = pl.ds(c * rows_chunk, rows_chunk)
            val = lax.dot_general(e_bf[rows, :], h_tile, (((1,), (1,)), ((), ())), preferred_element_type=jnp.float32)
            for d in range(n_dp):
                sub = val[d * piece : (d + 1) * piece]
                if not whole(c, d):
                    sub = jnp.where(iota_p + first_row(c, d) < block_rows, sub, NEG_BIG)
                for i, at in enumerate(ats):
                    logit[pl.ds(c * rows_chunk + d * piece, piece), at] = sub[:, i * LANE : (i + 1) * LANE]
                top = jnp.maximum(top, jnp.max(sub.reshape(piece // 8, 8, wide_tile), axis=0))
        top = jnp.max(top, axis=0, keepdims=True)
        for i, at in enumerate(ats):
            peak = top[:, i * LANE : (i + 1) * LANE]
            total = jnp.zeros((8, LANE), jnp.float32)
            for c in range(n_chunk):
                val = jnp.exp(logit[pl.ds(c * rows_chunk, rows_chunk), at] - peak)
                total = total + jnp.sum(val.reshape(rows_chunk // 8, 8, LANE), axis=0)
            lse[:, at] = peak + jnp.log(jnp.sum(total, axis=0, keepdims=True))

    def h_only(it, _):
        for k in range(per_tile):
            h_slot(it * per_tile + k)
        return 0

    def h_and_logits(it, _):
        j = it - lag
        for k in range(per_tile):
            h_slot(it * per_tile + k)
            x_slot((it - x_first) * per_tile + k)
            if k < 2:
                logit_pair(k * half_tok + j * LANE, k * half_tok + tok_a + j * LANE)
        return 0

    prepare_rows()
    lax.fori_loop(0, lag, h_only, 0)
    lax.fori_loop(lag, n_it, h_and_logits, 0)
    logit_pair((tiles_a - 1) * LANE, half_tok + (tiles_a - 1) * LANE)
    x_done = n_it - x_first

    def lse_copy(axis, idx, size, gathered, stage, k):
        return remote(lse, gathered.at[k], lse_send.at[stage, k], lse_recv.at[stage, k], {axis: lax.rem(idx + k, size)})

    def lse_finish(copies, gathered, size):
        own = lse[...]
        for copy in copies:
            copy.wait()
        top = own
        for k in range(1, size):
            top = jnp.maximum(top, gathered[k])
        total = jnp.exp(own - top)
        for k in range(1, size):
            total = total + jnp.exp(gathered[k] - top)
        lse[...] = top + jnp.log(total)

    for stage, (axis, idx, size, gathered) in enumerate((("pp", me, n_pp, lse_a), ("tp", tpi, n_tp, lse_b))):
        copies = [lse_copy(axis, idx, size, gathered, stage, k) for k in range(1, size)]
        for copy in copies:
            copy.start()
        x_it(x_done + stage)
        lse_finish(copies, gathered, size)
    x_done += 2

    @pl.when(jnp.logical_not(src_h))
    def _():
        tok_copy(0, lab, 1).wait_recv()

    inv_tok = 1.0 / tok_count
    n_wide = tok_count // wide_tile
    iota_w = lax.broadcasted_iota(jnp.int32, (piece, wide_tile), 0)
    vocab_base = tpi * block_rows

    def dlog_chunk(c):
        def tile(t, _):
            at = pl.ds(pl.multiple_of(t * wide_tile, wide_tile), wide_tile)
            norm = lse[:, at]
            labels = in_block(lab[:, at] - vocab_base, block_rows)
            for d in range(n_dp):
                prob = jnp.exp(logit[pl.ds(c * rows_chunk + d * piece, piece), at] - norm)
                hit = iota_w == labels - first_row(c, d)
                dlog[pl.ds(d * piece, piece), at] = (jnp.where(hit, prob - 1.0, prob) * inv_tok).astype(jnp.bfloat16)
            return 0

        lax.fori_loop(0, n_wide, tile, 0)

    def times(tokens, add):
        def go(c):
            rows = pl.ds(c * rows_chunk, rows_chunk)
            val = jnp.dot(dlog[...], tokens[...], preferred_element_type=jnp.float32)
            part[rows, :] = part[rows, :] + val if add else val

        return go

    head = times(h_bf, False)
    look = times(x_bf, True)
    x_its = tiles_a + lag - 1
    for c in range(n_chunk):
        if x_done < x_its:
            x_it(x_done)
            x_done += 1
        dlog_chunk(c)
        head(c)
    while x_done < x_its:
        x_it(x_done)
        x_done += 1

    @pl.when(jnp.logical_not(src_x))
    def _():
        tok_copy(1, ids, 1).wait_recv()

    def narrow(t, _):
        at = pl.ds(pl.multiple_of(t * LANE, LANE), LANE)
        x_bf[at, :] = x_f[at, :].astype(jnp.bfloat16)
        return 0

    lax.fori_loop(0, tok_count // LANE, narrow, 0)

    def one_hot_chunk(c):
        def tile(t, _):
            at = pl.ds(pl.multiple_of(t * wide_tile, wide_tile), wide_tile)
            rows = in_block(ids[:, at] - vocab_base, block_rows)
            for d in range(n_dp):
                hit = iota_w == rows - first_row(c, d)
                dlog[pl.ds(d * piece, piece), at] = jnp.where(hit, 1.0, 0.0).astype(jnp.bfloat16)
            return 0

        lax.fori_loop(0, n_wide, tile, 0)

    up, down, far = lax.rem(dpi + 1, 4), lax.rem(dpi + 3, 4), lax.rem(dpi + 2, 4)
    hd = dim // 2

    def rows_of(c, d):
        return pl.ds(pl.multiple_of(c * rows_chunk + d * piece, 16), piece)

    def rs_one(c):
        return (
            remote(part.at[rows_of(c, far), pl.ds(0, hd)], rs_a.at[c, 0], rs_send.at[0, c, 0], rs_recv.at[0, c, 0], {"dp": up}),
            remote(part.at[rows_of(c, far), pl.ds(hd, hd)], rs_a.at[c, 1], rs_send.at[0, c, 1], rs_recv.at[0, c, 1], {"dp": down}),
        )

    def rs_two(c):
        return (
            remote(part.at[rows_of(c, up), :], rs_b.at[c, 0], rs_send.at[1, c, 0], rs_recv.at[1, c, 0], {"dp": up}),
            remote(part.at[rows_of(c, down), :], rs_b.at[c, 1], rs_send.at[1, c, 1], rs_recv.at[1, c, 1], {"dp": down}),
        )

    def merge(c):
        for copy in rs_one(c):
            copy.wait_recv()
        part[rows_of(c, up), pl.ds(0, hd)] += rs_a[c, 0]
        part[rows_of(c, down), pl.ds(hd, hd)] += rs_a[c, 1]
        for copy in rs_two(c):
            copy.start()

    rings = (
        ("pp", h_f, x, n_x, lambda q: q * 2 + core),
        ("dp", x_f, dpi, n_dp, lambda q: q),
    )

    def block(c, q, core_at, first=0, n=piece):
        color, s, count = chunks[c]
        return rings[color][1].at[pl.ds(pl.multiple_of(((q * 2 + core_at) * count + s) * piece + first, 8), n), :]

    def ring_copy(c, q, way, sem, first=0, n=piece):
        axis, _, idx, size, device = rings[chunks[c][0]]
        to = device(lax.rem(idx + (1 if way == 0 else size - 1), size))
        at = block(c, q, core, first, n)
        return remote(at, at, f_send.at[c, sem], f_recv.at[c, sem], {axis: to})

    def share(c, k):
        _, _, idx, size, _ = rings[chunks[c][0]]
        at = block(c, lax.rem(idx + k, size), core)
        return remote(at, at, p_send.at[c, k], p_recv.at[c, k], partner)

    cut = piece // 2

    def forwards(c):
        _, _, idx, size, _ = rings[chunks[c][0]]
        return (
            ring_copy(c, lax.rem(idx + size - 1, size), 0, 2, 0, cut),
            ring_copy(c, lax.rem(idx + 1, size), 1, 3, cut, piece - cut),
        )

    def owns(c):
        idx = rings[chunks[c][0]][2]
        return ring_copy(c, idx, 0, 0), ring_copy(c, idx, 1, 1)

    def gather_one(c):
        if c == 0:
            pl.semaphore_wait(ready, 5)
        for copy in owns(c):
            copy.start()
        share(c, 0).start()

    def gather_two(c):
        for own, forward, k in zip(owns(c), forwards(c), (3, 1), strict=True):
            own.wait_recv()
            forward.start()
            share(c, k).start()

    def gather_three(c):
        for copy in forwards(c):
            copy.wait_recv()
        share(c, 2).start()

    def gather_four(c):
        for k in range(4):
            share(c, k).wait()
        for copy in owns(c) + forwards(c):
            copy.wait_send()

    def final(c):
        for copy in rs_two(c):
            copy.wait_recv()
        val = part[rows_of(c, dpi), :] + rs_b[c, 0] + rs_b[c, 1]
        color, s, count = chunks[c]
        own = (rings[color][2] * 2 + core) * count + s
        rings[color][1][pl.ds(pl.multiple_of(own * piece, 8), piece), :] = val
        squares = val * val
        squares = jnp.sum(squares.reshape(piece // 8, 8, dim), axis=0)
        tile = squares[:, :LANE]
        for i in range(1, dim // LANE):
            tile = tile + squares[:, i * LANE : (i + 1) * LANE]
        sq[...] = tile if c == 0 else sq[...] + tile

    h_drain()
    x_drain()
    for device in (right, left, partner, {"dp": up}, {"dp": down}):
        pl.semaphore_signal(ready, inc=1, device_id=device, device_id_type=MESH)

    for c in range(n_chunk + 4):
        if c < n_chunk:
            one_hot_chunk(c)
            look(c)
            for copy in rs_one(c):
                copy.start()
        if 0 <= c - 2 < n_chunk:
            merge(c - 2)
        if 0 <= c - 4 < n_chunk:
            final(c - 4)
            gather_one(c - 4)
        if 0 <= c - 5 < n_chunk:
            gather_two(c - 5)
        if 0 <= c - 6 < n_chunk:
            gather_three(c - 6)

    at = 0
    for axis, idx, size in (("pp", me, n_pp), ("tp", tpi, n_tp), ("dp", dpi, n_dp)):
        sq_all[at + idx] = sq[...]
        copies = [
            remote(sq, sq_all.at[at + idx], sq_send.at[at + k], sq_recv.at[at + k], {axis: lax.rem(idx + k, size)}) for k in range(1, size)
        ]
        for copy in copies:
            copy.start()
        if at == 0:
            gather_two(n_chunk - 1)
            gather_three(n_chunk - 2)
        for copy in copies:
            copy.wait()
        total = sq_all[at]
        for k in range(1, size):
            total = total + sq_all[at + k]
        sq[...] = total
        at += size
    gather_three(n_chunk - 1)
    total = jnp.sum(jnp.sum(sq[...], axis=0, keepdims=True), axis=1, keepdims=True) * (1.0 / (n_dp * n_dp))
    factor = (CLIP_NORM / jnp.maximum(jnp.sqrt(total), CLIP_NORM)) * (1.0 / n_dp)
    fac[...] = jnp.broadcast_to(factor, fac.shape)
    last = [pltpu.make_async_copy(fac, factor_out, out_sem.at[4])]
    for c in range(n_chunk):
        gather_four(c)
    for color in range(2):
        n = group_outs[2 * color].shape[0]
        for k, which in enumerate((core, 1 - core)):
            at = pl.ds(pl.multiple_of(which * n, 8), n)
            last.append(pltpu.make_async_copy(rings[color][1].at[at, :], group_outs[2 * color + k], out_sem.at[2 * color + k]))
    for copy in last:
        copy.start()

    for which, is_src, tok in ((0, src_h, lab), (1, src_x, ids)):

        @pl.when(is_src)
        def _(which=which, tok=tok):
            for k in range(1, n_pp):
                tok_copy(which, tok, k).wait_send()

    for c in range(n_chunk):
        for copy in rs_one(c) + rs_two(c):
            copy.wait_send()
    for copy in last:
        copy.wait()


def reduced_shards(master, acts, toks, sizes, chunks, bases, piece):
    n_tp, n_dp, n_pp = sizes
    block_rows, dim = master.shape
    tok_count = acts.shape[0]
    n_chunk = len(chunks)
    rows = n_chunk * n_dp * piece
    halves = [half_rows(sizes, chunks, piece, color) for color in (0, 0, 1, 1)]
    pieces = (tok_count // 2 // LANE + 1) // 2 * (LANE // PIECE_TOK)
    dma = pltpu.SemaphoreType.DMA
    f32, bf16 = jnp.float32, jnp.bfloat16
    outs = pl.pallas_call(
        functools.partial(front_kernel, (n_tp, n_dp, n_pp, chunks, bases, piece, block_rows)),
        out_shape=tuple(jax.ShapeDtypeStruct((n, dim), f32) for n in halves) + (jax.ShapeDtypeStruct((8, LANE), f32),),
        in_specs=[ANY, ANY, ANY],
        out_specs=(ANY,) * 5,
        scratch_shapes=[
            pltpu.VMEM((tok_count, dim), f32),
            pltpu.VMEM((tok_count, dim), f32),
            pltpu.VMEM((tok_count, dim), bf16),
            pltpu.VMEM((tok_count, dim), bf16),
            pltpu.VMEM((rows, dim), f32),
            pltpu.VMEM((rows, dim), bf16),
            pltpu.VMEM((rows, tok_count), f32),
            pltpu.VMEM((n_dp * piece, tok_count), bf16),
            pltpu.VMEM((1, tok_count), f32),
            pltpu.VMEM((n_pp, 1, tok_count), f32),
            pltpu.VMEM((n_tp, 1, tok_count), f32),
            pltpu.VMEM((n_chunk, 2, piece, dim // 2), f32),
            pltpu.VMEM((n_chunk, 2, piece, dim), f32),
            pltpu.VMEM((1, tok_count), jnp.int32),
            pltpu.VMEM((1, tok_count), jnp.int32),
            pltpu.VMEM((8, LANE), f32),
            pltpu.VMEM((n_pp + n_tp + n_dp, 8, LANE), f32),
            pltpu.VMEM((8, LANE), f32),
            dma((n_chunk,)),
            dma((2,)),
            dma((2, n_pp)),
            dma((2,)),
            dma((2, 4, pieces)),
            dma((2, 4)),
            dma((2, 2)),
            dma((2, 2)),
            dma((2, n_pp)),
            dma((2, n_pp)),
            dma((2, n_chunk, 2)),
            dma((2, n_chunk, 2)),
            dma((n_pp + n_tp + n_dp,)),
            dma((n_pp + n_tp + n_dp,)),
            dma((5,)),
            dma((n_chunk, 4)),
            dma((n_chunk, 4)),
            dma((n_chunk, 4)),
            dma((n_chunk, 4)),
            pltpu.SemaphoreType.REGULAR,
        ],
        compiler_params=pltpu.CompilerParams(collective_id=1, has_side_effects=True, vmem_limit_bytes=62 * 2**20),
        cost_estimate=pl.CostEstimate(flops=20 * 10**9, bytes_accessed=25 * 10**6, transcendentals=8 * 10**6),
        name="reduced_shards",
    )(master, acts, toks)
    return outs[:-1], outs[-1]


def adamw_kernel(n_prev, firsts, factor, *refs):
    n_seg = len(firsts)
    grads = refs[:n_seg]
    master, avg, avg_sq = refs[n_seg : n_seg + 3]
    new_master, new_avg, new_sq, new_bf = refs[n_seg + 3 + n_prev :]
    step = pl.program_id(0)
    g = grads[0][...]
    for first, ref in zip(firsts[1:], grads[1:], strict=True):
        g = jnp.where(step >= first, ref[...], g)
    g = g * factor[0:1, 0:1]
    m = BETA_ONE * avg[...] + (1.0 - BETA_ONE) * g
    v = BETA_TWO * avg_sq[...] + (1.0 - BETA_TWO) * g * g
    step_dir = (m * (1.0 / (1.0 - BETA_ONE**OPT_STEP))) / (jnp.sqrt(v * (1.0 / (1.0 - BETA_TWO**OPT_STEP))) + ADAM_EPS)
    w = master[...]
    w = w - LEARN_RATE * (step_dir + WEIGHT_DECAY * w)
    new_master[...] = w
    new_avg[...] = m
    new_sq[...] = v
    new_bf[...] = w.astype(jnp.bfloat16)


def update_rows(factor, segments, master, avg, avg_sq, prev, tile):
    block_rows, dim = master.shape
    counts = [-(-g.shape[0] // tile) for g, _ in segments]
    firsts = [sum(counts[:k]) for k in range(len(counts))]

    def local(k, i):
        rows = segments[k][0].shape[0]
        valid = jnp.minimum(rows, block_rows - segments[k][1]())
        return jnp.minimum(jnp.clip(i - firsts[k], 0, counts[k] - 1) * tile, valid - tile)

    def grad_index(k):
        return lambda i: (pl.multiple_of(local(k, i), 8), 0)

    def table_index(i):
        row = segments[0][1]() + local(0, i)
        for k in range(1, len(segments)):
            row = jnp.where(i >= firsts[k], segments[k][1]() + local(k, i), row)
        return pl.multiple_of(row, 8), 0

    shape = (pl.Element(tile), pl.Element(dim))
    table = pl.BlockSpec(shape, table_index)
    n_prev, n_seg = len(prev), len(segments)
    rows = sum(g.shape[0] for g, _ in segments)
    return pl.pallas_call(
        functools.partial(adamw_kernel, n_prev, firsts),
        grid=(sum(counts),),
        out_shape=(
            jax.ShapeDtypeStruct(master.shape, jnp.float32),
            jax.ShapeDtypeStruct(master.shape, jnp.float32),
            jax.ShapeDtypeStruct(master.shape, jnp.float32),
            jax.ShapeDtypeStruct(master.shape, jnp.bfloat16),
        ),
        in_specs=[pl.BlockSpec((8, LANE), lambda i: (0, 0))] + [pl.BlockSpec(shape, grad_index(k)) for k in range(n_seg)] + [table] * 3 + [ANY] * n_prev,
        out_specs=(table, table, table, table),
        input_output_aliases={4 + n_seg + i: i for i in range(n_prev)},
        compiler_params=pltpu.CompilerParams(vmem_limit_bytes=14 * 2**20),
        cost_estimate=pl.CostEstimate(flops=rows * dim * 2000, bytes_accessed=rows * dim * 30, transcendentals=rows * dim),
    )(factor, *[g for g, _ in segments], master, avg, avg_sq, *prev)


def half_rows(sizes, chunks, piece, color):
    _, n_dp, n_pp = sizes
    owners = n_pp if color == 0 else 2 * n_dp
    return owners // 2 * piece * sum(1 for k, _, _ in chunks if k == color)


def layout_of(block_rows, n_dp, n_pp):
    devices = n_dp * n_pp
    colors = (0, 1, 0, 1, 0)
    piece = -(-(-(-block_rows // (devices * len(colors)))) // 16) * 16
    chunks = tuple((k, colors[:i].count(k), colors.count(k)) for i, k in enumerate(colors))
    return piece, chunks, (0, devices * piece * colors.count(0))


def solution(mesh):
    n_tp, n_dp, n_pp = mesh.shape["tp"], mesh.shape["dp"], mesh.shape["pp"]
    n_x = n_pp // 2
    table_spec = P("tp", None)
    places = [(d, p) for d in range(n_dp) for p in range(n_pp)]

    def step_way(p):
        return 1 if p % 2 == 0 else -1

    col_ring = [(d * n_pp + p, (d + step_way(p)) % n_dp * n_pp + p) for d, p in places]
    row_ring = [(p, (p // 2 + step_way(p)) % n_x * 2 + p % 2) for p in range(n_pp)]
    swap = [(p, p ^ 1) for p in range(n_pp)]

    def along(color, val):
        return lax.ppermute(val, ("dp", "pp"), col_ring) if color == 0 else lax.ppermute(val, "pp", row_ring)

    def swapped(val):
        return lax.ppermute(val, "pp", swap)

    def device_step(master, exp_avg, exp_avg_sq, stage_ids, stage_acts):
        block_rows, dim = master.shape
        sizes = (n_tp, n_dp, n_pp)
        piece, chunks, bases = layout_of(block_rows, n_dp, n_pp)
        tok_count = stage_ids.shape[1] * stage_ids.shape[2]
        toks = stage_ids.reshape(1, tok_count)
        acts = stage_acts.reshape(tok_count, dim)
        groups, factor = reduced_shards(master, acts, toks, sizes, chunks, bases, piece)
        halves = [half_rows(sizes, chunks, piece, color) for color in range(2)]

        def segment(color, val, away, other):
            half = halves[color]

            def row():
                p = lax.axis_index("pp")
                core = lax.rem(p, 2)
                size = n_dp if color == 0 else n_x
                own = lax.axis_index("dp") if color == 0 else p // 2
                shift = away if away in (0, 2) else (2 * core - 1) * away
                group = lax.rem(own + shift + size, size)
                return bases[color] + (group * 2 + (1 - core if other else core)) * half

            return val, row

        first, second = groups[0::2], groups[1::2]
        ring_first = [along(k, first[k]) for k in range(2)]
        ring_second = [along(k, second[k]) for k in range(2)]
        swap_first = [swapped(ring_first[k]) for k in range(2)]
        far = [along(k, ring_first[k]) for k in range(2)]
        swap_second = [swapped(ring_second[k]) for k in range(2)]
        swap_far = [swapped(far[k]) for k in range(2)]
        spare = block_rows - bases[1] - (2 * n_x - 1) * halves[1]
        tile = min(160, spare // 8 * 8)
        plan = (
            [segment(k, v[k], 0, o) for o, v in ((False, first), (True, second)) for k in range(2)],
            [segment(k, ring_first[k], 1, False) for k in range(2)],
            [segment(k, swap_first[k], -1, True) for k in range(2)],
            [segment(k, ring_second[k], 1, True) for k in range(2)],
            [segment(k, swap_second[k], -1, False) for k in range(2)],
            [segment(k, far[k], 2, False) for k in range(2)],
            [segment(k, swap_far[k], 2, True) for k in range(2)],
        )
        outs = ()
        for segments in plan:
            outs = tuple(update_rows(factor, segments, master, exp_avg, exp_avg_sq, outs, tile))
        return outs

    specs = (table_spec, table_spec, table_spec, P("pp", "dp", None), P("pp", "dp", None, None))

    return jax.shard_map(device_step, mesh=mesh, in_specs=specs, out_specs=(table_spec,) * 4, check_vma=False)
```

profile of v0, /device:TPU:1, one launch (start us, length us, event | category | flops | bytes accessed | tf_op | source)
XLA Modules:
  0.0 408.4 jit_solution(8235703009925063559)
XLA Ops:
  0.6 172.3 %reduced_shards.1 = (f32[960,768]{1,0:T(8,128)}, f32[960,768]{1,0:T(8,128)}, f32[640,768]{1,0:T(8,128)}, f32[640,768]{1,0:T(8,128)}, f32[8,128]{1,0:T(8,128)}) custom-call(f32[12576,768]{1,0:T(8,128)} %refs_2_.11, bf16[2304,768]{1,0:T(8,128)(2,1)} %bitcast.2, s32[1,2304]{1,0:T(1,128)} %bitcast.3), custom_call_target="tpu_custom_call" | custom-call | flops 20000000000 | bytes 25000000 | tf_op jit(solution)/shard_map/reduced_shards/pallas_call | solution.py:535
  173.0 1.5 collective-permute-start
  174.5 3.1 collective-permute-start.3
  177.6 0.3 collective-permute-start.6
  177.9 29.6 %collective-permute-done.refs_0_ = f32[960,768]{1,0:T(8,128)S(1)} collective-permute-done((f32[960,768]{1,0:T(8,128)}, f32[960,768]{1,0:T(8,128)S(1)}, u32[]{:S(2)}, u32[]{:S(2)}) %collective-permute-start) | collective-permute-done | bytes 2949152 | tf_op jit(solution)/shard_map/ppermute | solution.py:676
  207.5 2.4 collective-permute-start.1
  209.9 3.1 collective-permute-start.8
  213.1 0.2 collective-permute-start.4
  213.3 21.7 %collective-permute-done.8.refs_1_ = f32[640,768]{1,0:T(8,128)} collective-permute-done((f32[640,768]{1,0:T(8,128)}, f32[640,768]{1,0:T(8,128)}, u32[]{:S(2)}, u32[]{:S(2)}) %collective-permute-start.8) | collective-permute-done | bytes 1966112 | tf_op jit(solution)/shard_map/ppermute | solution.py:676
  234.9 1.4 collective-permute-start.10
  236.4 2.9 collective-permute-done.6.refs_0_
  239.3 2.2 collective-permute-start.7
  241.5 29.4 %collective-permute-done.1.refs_0_ = f32[960,768]{1,0:T(8,128)} collective-permute-done((f32[960,768]{1,0:T(8,128)S(1)}, f32[960,768]{1,0:T(8,128)}, u32[]{:S(2)}, u32[]{:S(2)}) %collective-permute-start.1) | collective-permute-done | bytes 2949152 | tf_op jit(solution)/shard_map/ppermute | solution.py:676
  270.9 2.2 collective-permute-start.2
  273.1 0.0 collective-permute-start.9
  273.1 0.0 collective-permute-done.4.refs_1_
  273.1 0.5 collective-permute-start.5
  273.6 1.8 copy-done
  275.4 1.8 copy-done.1
  277.2 1.5 copy-done.2
  278.8 1.5 copy-done.3
  280.3 0.7 copy-done.4
  281.0 30.1 %shard_map.84 = (f32[12576,768]{1,0:T(8,128)}, f32[12576,768]{1,0:T(8,128)}, f32[12576,768]{1,0:T(8,128)}, bf16[12576,768]{1,0:T(8,128)(2,1)}) custom-call(f32[8,128]{1,0:T(8,128)S(1)} %copy-done.4, f32[960,768]{1,0:T(8,128)S(1)} %copy-done, f32[640,768]{1,0:T(8,128)S(1)} %copy-done.2, f32[960,768]{1,0:T(8,128)S(1)} %copy-done.1, f32[640,768]{1,0:T(8,128)S(1)} %copy-done.3, ...), custom_call_target="tpu_custom_call" | custom-call | flops 4915200000 | bytes 73728000 | tf_op jit(solution)/shard_map/pallas_call | solution.py:631
  311.1 15.6 %shard_map.85 = (f32[12576,768]{1,0:T(8,128)}, f32[12576,768]{1,0:T(8,128)}, f32[12576,768]{1,0:T(8,128)}, bf16[12576,768]{1,0:T(8,128)(2,1)}) custom-call(f32[8,128]{1,0:T(8,128)S(1)} %copy-done.4, f32[960,768]{1,0:T(8,128)S(1)} %collective-permute-done.refs_0_, ...), custom_call_target="tpu_custom_call", output_to_operand_aliasing={{0}: (6, {}), {1}: (7, {}), {2}: (8, {}), {3}: (9, {})} | custom-call | flops 2457600000 | bytes 36864000 | tf_op jit(solution)/shard_map/pallas_call | solution.py:631
  326.7 0.0 collective-permute-done.10.refs_0_
  326.7 15.6 %shard_map.86 = (f32[12576,768]{1,0:T(8,128)}, f32[12576,768]{1,0:T(8,128)}, f32[12576,768]{1,0:T(8,128)}, bf16[12576,768]{1,0:T(8,128)(2,1)}) custom-call(f32[8,128]{1,0:T(8,128)S(1)} %copy-done.4, f32[960,768]{1,0:T(8,128)S(1)} %collective-permute-done.10.refs_0_, ...), custom_call_target="tpu_custom_call", output_to_operand_aliasing={{0}: (6, {}), {1}: (7, {}), {2}: (8, {}), {3}: (9, {})} | custom-call | flops 2457600000 | bytes 36864000 | tf_op jit(solution)/shard_map/pallas_call | solution.py:631
  342.3 16.5 %shard_map.87 = (f32[12576,768]{1,0:T(8,128)}, f32[12576,768]{1,0:T(8,128)}, f32[12576,768]{1,0:T(8,128)}, bf16[12576,768]{1,0:T(8,128)(2,1)}) custom-call(f32[8,128]{1,0:T(8,128)S(1)} %copy-done.4, f32[960,768]{1,0:T(8,128)} %collective-permute-done.6.refs_0_, ...), custom_call_target="tpu_custom_call", output_to_operand_aliasing={{0}: (6, {}), {1}: (7, {}), {2}: (8, {}), {3}: (9, {})} | custom-call | flops 2457600000 | bytes 36864000 | tf_op jit(solution)/shard_map/pallas_call | solution.py:631
  358.8 0.0 collective-permute-done.9.refs_1_
  358.8 16.4 %shard_map.88 = (f32[12576,768]{1,0:T(8,128)}, f32[12576,768]{1,0:T(8,128)}, f32[12576,768]{1,0:T(8,128)}, bf16[12576,768]{1,0:T(8,128)(2,1)}) custom-call(f32[8,128]{1,0:T(8,128)S(1)} %copy-done.4, f32[960,768]{1,0:T(8,128)} %collective-permute-done.7.refs_0_, ...), custom_call_target="tpu_custom_call", output_to_operand_aliasing={{0}: (6, {}), {1}: (7, {}), {2}: (8, {}), {3}: (9, {})} | custom-call | flops 2457600000 | bytes 36864000 | tf_op jit(solution)/shard_map/pallas_call | solution.py:631
  375.2 16.6 %shard_map.89 = (f32[12576,768]{1,0:T(8,128)}, f32[12576,768]{1,0:T(8,128)}, f32[12576,768]{1,0:T(8,128)}, bf16[12576,768]{1,0:T(8,128)(2,1)}) custom-call(f32[8,128]{1,0:T(8,128)S(1)} %copy-done.4, f32[960,768]{1,0:T(8,128)} %collective-permute-done.1.refs_0_, ...), custom_call_target="tpu_custom_call", output_to_operand_aliasing={{0}: (6, {}), {1}: (7, {}), {2}: (8, {}), {3}: (9, {})} | custom-call | flops 2457600000 | bytes 36864000 | tf_op jit(solution)/shard_map/pallas_call | solution.py:631
  391.8 0.0 collective-permute-done.2.refs_0_
  391.8 16.6 %shard_map.90 = (f32[12576,768]{1,0:T(8,128)}, f32[12576,768]{1,0:T(8,128)}, f32[12576,768]{1,0:T(8,128)}, bf16[12576,768]{1,0:T(8,128)(2,1)}) custom-call(f32[8,128]{1,0:T(8,128)S(1)} %copy-done.4, f32[960,768]{1,0:T(8,128)} %collective-permute-done.2.refs_0_, ...), custom_call_target="tpu_custom_call", output_to_operand_aliasing={{0}: (6, {}), {1}: (7, {}), {2}: (8, {}), {3}: (9, {})} | custom-call | flops 2457600000 | bytes 36864000 | tf_op jit(solution)/shard_map/pallas_call | solution.py:631
  (10 shorter events, 0.0 us)
Async XLA Ops:
  173.0 34.6 %collective-permute-start = (f32[960,768]{1,0:T(8,128)}, f32[960,768]{1,0:T(8,128)S(1)}, u32[]{:S(2)}, u32[]{:S(2)}) collective-permute-start(f32[960,768]{1,0:T(8,128)} %get-tuple-element.34.refs_0_), channel_id=1, source_target_pairs={{0,8},{1,25},{2,10},{3,27},{4,12},{5,29},{6,14},{7,31},{8,16},{9,1... | collective-permute-start | bytes 8847368 | tf_op jit(solution)/shard_map/ppermute | solution.py:676
  174.5 38.6 %collective-permute-start.3 = (f32[640,768]{1,0:T(8,128)}, f32[640,768]{1,0:T(8,128)S(1)}, u32[]{:S(2)}, u32[]{:S(2)}) collective-permute-start(f32[640,768]{1,0:T(8,128)} %get-tuple-element.35.refs_1_), channel_id=1, source_target_pairs={{0,2},{1,7},{2,4},{3,1},{4,6},{5,3},{6,0},{7,5},{8,10},{9,15},{10,... | collective-permute-start | bytes 5898248 | tf_op jit(solution)/shard_map/ppermute | solution.py:676
  177.6 61.6 %collective-permute-start.6 = (f32[960,768]{1,0:T(8,128)}, f32[960,768]{1,0:T(8,128)}, u32[]{:S(2)}, u32[]{:S(2)}) collective-permute-start(f32[960,768]{1,0:T(8,128)} %get-tuple-element.36.refs_2_), channel_id=1, source_target_pairs={{0,8},{1,25},{2,10},{3,27},{4,12},{5,29},{6,14},{7,31},{8,16},{9,1... | collective-permute-start | bytes 8847368 | tf_op jit(solution)/shard_map/ppermute | solution.py:676
  207.5 63.3 %collective-permute-start.1 = (f32[960,768]{1,0:T(8,128)S(1)}, f32[960,768]{1,0:T(8,128)}, u32[]{:S(2)}, u32[]{:S(2)}) collective-permute-start(f32[960,768]{1,0:T(8,128)S(1)} %collective-permute-done.refs_0_), channel_id=1, source_target_pairs={{0,8},{1,25},{2,10},{3,27},{4,12},{5,29},{6,14},{7,31},{8,16},{9,1... | collective-permute-start | bytes 8847368 | tf_op jit(solution)/shard_map/ppermute | solution.py:676
  209.9 25.0 %collective-permute-start.8 = (f32[640,768]{1,0:T(8,128)}, f32[640,768]{1,0:T(8,128)}, u32[]{:S(2)}, u32[]{:S(2)}) collective-permute-start(f32[640,768]{1,0:T(8,128)} %get-tuple-element.37.refs_3_), channel_id=1, source_target_pairs={{0,2},{1,7},{2,4},{3,1},{4,6},{5,3},{6,0},{7,5},{8,10},{9,15},{10,... | collective-permute-start | bytes 5898248 | tf_op jit(solution)/shard_map/ppermute | solution.py:676
  213.1 60.0 %collective-permute-start.11 = (f32[640,768]{1,0:T(8,128)S(1)}, f32[640,768]{1,0:T(8,128)S(1)}, u32[]{:S(2)}, u32[]{:S(2)}) collective-permute-start(f32[640,768]{1,0:T(8,128)S(1)} %collective-permute-done.3.refs_1_), channel_id=1, source_target_pairs={{0,1},{1,0},{2,3},{3,2},{4,5},{5,4},{6,7},{7,6},{8,9},{9,8},{10,11... | collective-permute-start | bytes 5898248 | tf_op jit(solution)/shard_map/ppermute | solution.py:679
  213.1 60.0 %collective-permute-start.4 = (f32[640,768]{1,0:T(8,128)S(1)}, f32[640,768]{1,0:T(8,128)}, u32[]{:S(2)}, u32[]{:S(2)}) collective-permute-start(f32[640,768]{1,0:T(8,128)S(1)} %collective-permute-done.3.refs_1_), channel_id=1, source_target_pairs={{0,2},{1,7},{2,4},{3,1},{4,6},{5,3},{6,0},{7,5},{8,10},{9,15},{10,... | collective-permute-start | bytes 5898248 | tf_op jit(solution)/shard_map/ppermute | solution.py:676
  234.9 91.8 %collective-permute-start.10 = (f32[960,768]{1,0:T(8,128)S(1)}, f32[960,768]{1,0:T(8,128)S(1)}, u32[]{:S(2)}, u32[]{:S(2)}) collective-permute-start(f32[960,768]{1,0:T(8,128)S(1)} %collective-permute-done.refs_0_), channel_id=1, source_target_pairs={{0,1},{1,0},{2,3},{3,2},{4,5},{5,4},{6,7},{7,6},{8,9},{9,8},{10,11... | collective-permute-start | bytes 8847368 | tf_op jit(solution)/shard_map/ppermute | solution.py:679
  239.3 119.6 %collective-permute-start.7 = (f32[960,768]{1,0:T(8,128)}, f32[960,768]{1,0:T(8,128)}, u32[]{:S(2)}, u32[]{:S(2)}) collective-permute-start(f32[960,768]{1,0:T(8,128)} %collective-permute-done.6.refs_0_), channel_id=1, source_target_pairs={{0,1},{1,0},{2,3},{3,2},{4,5},{5,4},{6,7},{7,6},{8,9},{9,8},{10,11... | collective-permute-start | bytes 8847368 | tf_op jit(solution)/shard_map/ppermute | solution.py:679
  270.9 121.0 %collective-permute-start.2 = (f32[960,768]{1,0:T(8,128)}, f32[960,768]{1,0:T(8,128)}, u32[]{:S(2)}, u32[]{:S(2)}) collective-permute-start(f32[960,768]{1,0:T(8,128)} %collective-permute-done.1.refs_0_), channel_id=1, source_target_pairs={{0,1},{1,0},{2,3},{3,2},{4,5},{5,4},{6,7},{7,6},{8,9},{9,8},{10,11... | collective-permute-start | bytes 8847368 | tf_op jit(solution)/shard_map/ppermute | solution.py:679
  273.1 85.7 %collective-permute-start.9 = (f32[640,768]{1,0:T(8,128)}, f32[640,768]{1,0:T(8,128)}, u32[]{:S(2)}, u32[]{:S(2)}) collective-permute-start(f32[640,768]{1,0:T(8,128)} %collective-permute-done.8.refs_1_), channel_id=1, source_target_pairs={{0,1},{1,0},{2,3},{3,2},{4,5},{5,4},{6,7},{7,6},{8,9},{9,8},{10,11... | collective-permute-start | bytes 5898248 | tf_op jit(solution)/shard_map/ppermute | solution.py:679
  273.1 118.8 %collective-permute-start.5 = (f32[640,768]{1,0:T(8,128)}, f32[640,768]{1,0:T(8,128)}, u32[]{:S(2)}, u32[]{:S(2)}) collective-permute-start(f32[640,768]{1,0:T(8,128)} %collective-permute-done.4.refs_1_), channel_id=1, source_target_pairs={{0,1},{1,0},{2,3},{3,2},{4,5},{5,4},{6,7},{7,6},{8,9},{9,8},{10,11... | collective-permute-start | bytes 5898248 | tf_op jit(solution)/shard_map/ppermute | solution.py:679
  273.6 1.8 copy-start
  275.4 1.8 copy-start.1
  277.2 1.5 copy-start.2
  278.8 1.5 copy-start.3
  280.3 0.7 copy-start.4
where the time goes:
time: 411 us; the launch traced here: 408 us
  Pallas kernels  300 us (73%)
  waiting for transfers between devices  83.6 us (20%)
  starting transfers between devices  17 us (4%)
  local copies, waits for them, and re-layouts  7.44 us (2%)
    pallas_call x1, Pallas kernels, reduced_shards(): pl.pallas_call(functools.partial(front_kernel, (n_tp, n_dp, n_pp, chunks,...  172 us
    pallas_call x7, Pallas kernels, update_rows(): pl.pallas_call(functools.partial(adamw_kernel, n_prev, firsts), grid=(sum...  127 us
    ppermute x3, waiting for transfers between devices, along(): lax.ppermute(val, ('dp', 'pp'), col_ring)  61.9 us
    ppermute x3, waiting for transfers between devices, along(): lax.ppermute(val, 'pp', row_ring)  21.7 us
  transfers between devices with their start and end apart: 12, of which 4 were waited for; matrix products, arithmetic and copies ran while one was open for 0% of the time, Pallas kernels for 27%

commit v1 on v0

--- a/solution.py
+++ b/solution.py
@@ -114,31 +114,25 @@
         for k in range(1, size):
             pl.semaphore_signal(barrier, inc=1, device_id={axis: lax.rem(idx + k, size)}, device_id_type=MESH)
 
-    for is_src, buf, tok, wide in ((src_h, h_bf, lab, h_f), (src_x, x_bf, ids, x_f)):
-
-        @pl.when(is_src)
-        def _(buf=buf, tok=tok, wide=wide):
-            for c in source_loads(buf, tok):
-                c.wait()
-
-            def widen(t, _):
-                at = pl.ds(pl.multiple_of(t * LANE, LANE), LANE)
-                wide[at, :] = buf[at, :].astype(jnp.float32)
-                return 0
-
-            lax.fori_loop(0, tok_count // LANE, widen, 0)
+    def widen(buf, wide):
+        def one(t, _):
+            at = pl.ds(pl.multiple_of(t * LANE, LANE), LANE)
+            wide[at, :] = buf[at, :].astype(jnp.float32)
+            return 0
+
+        return one
+
+    @pl.when(src_h)
+    def _():
+        for c in source_loads(h_bf, lab):
+            c.wait()
+        for t in (0, tok_a, half_tok, half_tok + tok_a):
+            widen(h_bf, h_f)(t // LANE, 0)
 
     pl.semaphore_wait(barrier, n_pp + n_tp + n_dp - 3)
 
     def tok_copy(which, ref, k):
         return remote(ref, ref, tok_send.at[which, k], tok_recv.at[which], {"pp": lax.rem(me + k, n_pp)})
-
-    for which, is_src, tok in ((0, src_h, lab), (1, src_x, ids)):
-
-        @pl.when(is_src)
-        def _(which=which, tok=tok):
-            for k in range(1, n_pp):
-                tok_copy(which, tok, k).start()
 
     half = lax.rem(tpi, 2)
     partner = {"pp": x * 2 + 1 - core}
@@ -149,14 +143,15 @@
     hop = 2 * per_tile // 2
     lag = (hop * (n_x - 2) + hop) // per_tile + 1
 
-    def stream(s, buf):
+    def stream(s, buf, lead=0):
         handler = core == 1 - s
         u = lax.rem(x - (n_x - 1, 0)[s] + n_x, n_x)
         base = [half * half_tok, half * half_tok + tok_a, (1 - half) * half_tok, (1 - half) * half_tok + tok_a]
         ahead = jnp.maximum(u - 1, 0) * hop
         behind = jnp.where(u == 0, 0, (n_x - 1 - u) * hop)
         second = jnp.where(u == 0, 0, hop)
-        offs = (ahead, behind, ahead + second, behind + second)
+        early = jnp.where(handler & (u == 0), lead * per_tile, 0)
+        offs = (ahead - early, behind - early, ahead + second - early, behind + second - early)
 
         def rows(kind, p, n):
             return buf.at[pl.ds(pl.multiple_of(base[kind] + p * PIECE_TOK, PIECE_TOK), n), :]
@@ -202,9 +197,9 @@
         return slot, drain
 
     h_slot, h_drain = stream(0, h_f)
-    x_slot, x_drain = stream(1, x_f)
     n_it = lag + tiles_b
-    x_first = tiles_a
+    x_first = n_it - 1
+    x_slot, x_drain = stream(1, x_f, x_first - tiles_a)
 
     def x_it(it):
         for k in range(per_tile):
@@ -263,8 +258,32 @@
                 logit_pair(k * half_tok + j * LANE, k * half_tok + tok_a + j * LANE)
         return 0
 
+    @pl.when(src_h)
+    def _():
+        h_only(0, 0)
+        for t, n in ((0, tiles_a), (tiles_a, tiles_b), (tiles_a + tiles_b, tiles_a), (2 * tiles_a + tiles_b, tiles_b)):
+            lax.fori_loop(t + 1, t + n, widen(h_bf, h_f), 0)
+
     prepare_rows()
-    lax.fori_loop(0, lag, h_only, 0)
+
+    @pl.when(src_x)
+    def _():
+        for c in source_loads(x_bf, ids):
+            c.wait()
+        lax.fori_loop(0, tok_count // LANE, widen(x_bf, x_f), 0)
+
+    for which, is_src, tok in ((0, src_h, lab), (1, src_x, ids)):
+
+        @pl.when(is_src)
+        def _(which=which, tok=tok):
+            for k in range(1, n_pp):
+                tok_copy(which, tok, k).start()
+
+    @pl.when(jnp.logical_not(src_h))
+    def _():
+        h_only(0, 0)
+
+    lax.fori_loop(1, lag, h_only, 0)
     lax.fori_loop(lag, n_it, h_and_logits, 0)
     logit_pair((tiles_a - 1) * LANE, half_tok + (tiles_a - 1) * LANE)
     x_done = n_it - x_first
@@ -498,15 +517,16 @@
     factor = (CLIP_NORM / jnp.maximum(jnp.sqrt(total), CLIP_NORM)) * (1.0 / n_dp)
     fac[...] = jnp.broadcast_to(factor, fac.shape)
     last = [pltpu.make_async_copy(fac, factor_out, out_sem.at[4])]
-    for c in range(n_chunk):
-        gather_four(c)
+    last[0].start()
     for color in range(2):
+        for c in range(n_chunk):
+            if chunks[c][0] == color:
+                gather_four(c)
         n = group_outs[2 * color].shape[0]
         for k, which in enumerate((core, 1 - core)):
             at = pl.ds(pl.multiple_of(which * n, 8), n)
             last.append(pltpu.make_async_copy(rings[color][1].at[at, :], group_outs[2 * color + k], out_sem.at[2 * color + k]))
-    for copy in last:
-        copy.start()
+            last[-1].start()
 
     for which, is_src, tok in ((0, src_h, lab), (1, src_x, ids)):
 
@@ -584,25 +604,41 @@
     return outs[:-1], outs[-1]
 
 
+def in_hbm(val):
+    return pltpu.with_memory_space_constraint(val, pltpu.HBM)
+
+
+SLAB = 16
+
+
 def adamw_kernel(n_prev, firsts, factor, *refs):
     n_seg = len(firsts)
     grads = refs[:n_seg]
     master, avg, avg_sq = refs[n_seg : n_seg + 3]
     new_master, new_avg, new_sq, new_bf = refs[n_seg + 3 + n_prev :]
     step = pl.program_id(0)
-    g = grads[0][...]
-    for first, ref in zip(firsts[1:], grads[1:], strict=True):
-        g = jnp.where(step >= first, ref[...], g)
-    g = g * factor[0:1, 0:1]
-    m = BETA_ONE * avg[...] + (1.0 - BETA_ONE) * g
-    v = BETA_TWO * avg_sq[...] + (1.0 - BETA_TWO) * g * g
-    step_dir = (m * (1.0 / (1.0 - BETA_ONE**OPT_STEP))) / (jnp.sqrt(v * (1.0 / (1.0 - BETA_TWO**OPT_STEP))) + ADAM_EPS)
-    w = master[...]
-    w = w - LEARN_RATE * (step_dir + WEIGHT_DECAY * w)
-    new_master[...] = w
-    new_avg[...] = m
-    new_sq[...] = v
-    new_bf[...] = w.astype(jnp.bfloat16)
+    scale = factor[0:1, 0:1]
+    rows, _ = new_master.shape
+    slab = min(SLAB, rows)
+
+    def some_rows(i, _):
+        at = pl.ds(pl.multiple_of(i * slab, slab), slab)
+        g = grads[0][at, :]
+        for first, ref in zip(firsts[1:], grads[1:], strict=True):
+            g = jnp.where(step >= first, ref[at, :], g)
+        g = g * scale
+        m = BETA_ONE * avg[at, :] + (1.0 - BETA_ONE) * g
+        v = BETA_TWO * avg_sq[at, :] + (1.0 - BETA_TWO) * g * g
+        new_avg[at, :] = m
+        new_sq[at, :] = v
+        step_dir = (m * (1.0 / (1.0 - BETA_ONE**OPT_STEP))) / (jnp.sqrt(v * (1.0 / (1.0 - BETA_TWO**OPT_STEP))) + ADAM_EPS)
+        w = master[at, :]
+        w = w - LEARN_RATE * (step_dir + WEIGHT_DECAY * w)
+        new_master[at, :] = w
+        new_bf[at, :] = w.astype(jnp.bfloat16)
+        return 0
+
+    lax.fori_loop(0, rows // slab, some_rows, 0)
 
 
 def update_rows(factor, segments, master, avg, avg_sq, prev, tile):
@@ -642,7 +678,7 @@
         input_output_aliases={4 + n_seg + i: i for i in range(n_prev)},
         compiler_params=pltpu.CompilerParams(vmem_limit_bytes=14 * 2**20),
         cost_estimate=pl.CostEstimate(flops=rows * dim * 2000, bytes_accessed=rows * dim * 30, transcendentals=rows * dim),
-    )(factor, *[g for g, _ in segments], master, avg, avg_sq, *prev)
+    )(in_hbm(factor), *[g for g, _ in segments], *[in_hbm(v) for v in (master, avg, avg_sq)], *prev)
 
 
 def half_rows(sizes, chunks, piece, color):
@@ -653,7 +689,7 @@
 
 def layout_of(block_rows, n_dp, n_pp):
     devices = n_dp * n_pp
-    colors = (0, 1, 0, 1, 0)
+    colors = (0, 0, 1, 0, 1)
     piece = -(-(-(-block_rows // (devices * len(colors)))) // 16) * 16
     chunks = tuple((k, colors[:i].count(k), colors.count(k)) for i, k in enumerate(colors))
     return piece, chunks, (0, devices * piece * colors.count(0))
@@ -712,7 +748,7 @@
         spare = block_rows - bases[1] - (2 * n_x - 1) * halves[1]
         tile = min(160, spare // 8 * 8)
         plan = (
-            [segment(k, v[k], 0, o) for o, v in ((False, first), (True, second)) for k in range(2)],
+            [segment(k, in_hbm(v[k]), 0, o) for o, v in ((False, first), (True, second)) for k in range(2)],
             [segment(k, ring_first[k], 1, False) for k in range(2)],
             [segment(k, swap_first[k], -1, True) for k in range(2)],
             [segment(k, ring_second[k], 1, True) for k in range(2)],

time: 411 us -> 391 us (0.951)
  Pallas kernels: 300 us -> 286 us
  local copies, waits for them, and re-layouts: 7.44 us -> 0 us
    pallas_call x1, Pallas kernels: 172 us -> 153 us  [reduced_shards(): pl.pallas_call(functools.partial(front_kernel, (n_tp, n_dp, n_pp, chunks,...]
    unnamed x10 -> x0, local copies, waits for them, and re-layouts: 7.44 us -> none
    pallas_call x7, Pallas kernels: 127 us -> 133 us  [update_rows(): pl.pallas_call(functools.partial(adamw_kernel, n_prev, firsts), grid=(sum...]
  transfers between devices with their start and end apart: 12 -> 12, of which waited for: 4 -> 4; matrix products, arithmetic and copies ran while one was open for 0% -> 0% of each run, Pallas kernels for 27% -> 30%
where the time goes in v1:
time: 391 us; the launch traced here: 388 us
  Pallas kernels  286 us (73%)
  waiting for transfers between devices  81 us (21%)
  starting transfers between devices  20.4 us (5%)
    pallas_call x1, Pallas kernels, reduced_shards(): pl.pallas_call(functools.partial(front_kernel, (n_tp, n_dp, n_pp, chunks,...  153 us
    pallas_call x7, Pallas kernels, update_rows(): pl.pallas_call(functools.partial(adamw_kernel, n_prev, firsts), grid=(sum...  133 us
    ppermute x3, waiting for transfers between devices, along(): lax.ppermute(val, ('dp', 'pp'), col_ring)  60.2 us
    ppermute x3, waiting for transfers between devices, along(): lax.ppermute(val, 'pp', row_ring)  20.8 us
    ppermute x6, starting transfers between devices, swapped(): return lax.ppermute(val, 'pp', swap)  8.9 us
    ppermute x3, starting transfers between devices, along(): lax.ppermute(val, 'pp', row_ring)  7.88 us
  transfers between devices with their start and end apart: 12, of which 4 were waited for; matrix products, arithmetic and copies ran while one was open for 0% of the time, Pallas kernels for 30%

profile of v1, /device:TPU:1, one launch (start us, length us, event | category | flops | bytes accessed | tf_op | source)
XLA Modules:
  0.0 388.0 jit_solution(8215014667685511403)
XLA Ops:
  0.6 153.3 %reduced_shards.1 = (f32[960,768]{1,0:T(8,128)}, f32[960,768]{1,0:T(8,128)}, f32[640,768]{1,0:T(8,128)}, f32[640,768]{1,0:T(8,128)}, f32[8,128]{1,0:T(8,128)}) custom-call(f32[12576,768]{1,0:T(8,128)} %refs_2_.11, bf16[2304,768]{1,0:T(8,128)(2,1)} %bitcast.2, s32[1,2304]{1,0:T(1,128)} %bitcast.3), custom_call_target="tpu_custom_call" | custom-call | flops 20000000000 | bytes 25000000 | tf_op jit(solution)/shard_map/reduced_shards/pallas_call | solution.py:555
  153.9 1.2 collective-permute-start
  155.2 3.4 collective-permute-start.3
  158.6 0.3 collective-permute-start.6
  158.9 29.6 %collective-permute-done.refs_0_ = f32[960,768]{1,0:T(8,128)S(1)} collective-permute-done((f32[960,768]{1,0:T(8,128)}, f32[960,768]{1,0:T(8,128)S(1)}, u32[]{:S(2)}, u32[]{:S(2)}) %collective-permute-start) | collective-permute-done | bytes 2949152 | tf_op jit(solution)/shard_map/ppermute | solution.py:712
  188.5 2.1 collective-permute-start.1
  190.6 3.4 collective-permute-start.8
  194.0 0.0 collective-permute-done.3.refs_1_
  194.0 0.0 collective-permute-start.11
  194.0 1.0 collective-permute-start.4
  195.1 20.8 %collective-permute-done.8.refs_1_ = f32[640,768]{1,0:T(8,128)} collective-permute-done((f32[640,768]{1,0:T(8,128)}, f32[640,768]{1,0:T(8,128)}, u32[]{:S(2)}, u32[]{:S(2)}) %collective-permute-start.8) | collective-permute-done | bytes 1966112 | tf_op jit(solution)/shard_map/ppermute | solution.py:712
  215.9 2.3 collective-permute-start.10
  218.2 2.0 collective-permute-done.6.refs_0_
  220.2 3.1 collective-permute-start.7
  223.3 28.5 %collective-permute-done.1.refs_0_ = f32[960,768]{1,0:T(8,128)} collective-permute-done((f32[960,768]{1,0:T(8,128)S(1)}, f32[960,768]{1,0:T(8,128)}, u32[]{:S(2)}, u32[]{:S(2)}) %collective-permute-start.1) | collective-permute-done | bytes 2949152 | tf_op jit(solution)/shard_map/ppermute | solution.py:712
  251.8 3.1 collective-permute-start.2
  254.9 0.0 collective-permute-done.11.refs_1_
  254.9 0.0 collective-permute-start.9
  254.9 0.0 collective-permute-done.4.refs_1_
  254.9 0.5 collective-permute-start.5
  255.4 32.1 %shard_map.84 = (f32[12576,768]{1,0:T(8,128)}, f32[12576,768]{1,0:T(8,128)}, f32[12576,768]{1,0:T(8,128)}, bf16[12576,768]{1,0:T(8,128)(2,1)}) custom-call(f32[8,128]{1,0:T(8,128)} %get-tuple-element.33.factor, f32[960,768]{1,0:T(8,128)} %get-tuple-element.34.refs_0_, f32[640,768]{1,0:T(8,128)} %get-tuple-element.35.refs_1_, ...), custom_call_target="tpu_custom_call" | custom-call | flops 4915200000 | bytes 73728000 | tf_op jit(solution)/shard_map/pallas_call | solution.py:667
  287.5 16.2 %shard_map.85 = (f32[12576,768]{1,0:T(8,128)}, f32[12576,768]{1,0:T(8,128)}, f32[12576,768]{1,0:T(8,128)}, bf16[12576,768]{1,0:T(8,128)(2,1)}) custom-call(f32[8,128]{1,0:T(8,128)} %get-tuple-element.33.factor, f32[960,768]{1,0:T(8,128)S(1)} %collective-permute-done.refs_0_, ...), custom_call_target="tpu_custom_call", output_to_operand_aliasing={{0}: (6, {}), {1}: (7, {}), {2}: (8, {}), {3}: (9, {})} | custom-call | flops 2457600000 | bytes 36864000 | tf_op jit(solution)/shard_map/pallas_call | solution.py:667
  303.7 0.0 collective-permute-done.10.refs_0_
  303.7 16.2 %shard_map.86 = (f32[12576,768]{1,0:T(8,128)}, f32[12576,768]{1,0:T(8,128)}, f32[12576,768]{1,0:T(8,128)}, bf16[12576,768]{1,0:T(8,128)(2,1)}) custom-call(f32[8,128]{1,0:T(8,128)} %get-tuple-element.33.factor, f32[960,768]{1,0:T(8,128)S(1)} %collective-permute-done.10.refs_0_, ...), custom_call_target="tpu_custom_call", output_to_operand_aliasing={{0}: (6, {}), {1}: (7, {}), {2}: (8, {}), {3}: (9, {})} | custom-call | flops 2457600000 | bytes 36864000 | tf_op jit(solution)/shard_map/pallas_call | solution.py:667
  319.9 17.1 %shard_map.87 = (f32[12576,768]{1,0:T(8,128)}, f32[12576,768]{1,0:T(8,128)}, f32[12576,768]{1,0:T(8,128)}, bf16[12576,768]{1,0:T(8,128)(2,1)}) custom-call(f32[8,128]{1,0:T(8,128)} %get-tuple-element.33.factor, f32[960,768]{1,0:T(8,128)} %collective-permute-done.6.refs_0_, ...), custom_call_target="tpu_custom_call", output_to_operand_aliasing={{0}: (6, {}), {1}: (7, {}), {2}: (8, {}), {3}: (9, {})} | custom-call | flops 2457600000 | bytes 36864000 | tf_op jit(solution)/shard_map/pallas_call | solution.py:667
  337.0 0.0 collective-permute-done.9.refs_1_
  337.0 0.0 collective-permute-done.7.refs_0_
  337.0 16.7 %shard_map.88 = (f32[12576,768]{1,0:T(8,128)}, f32[12576,768]{1,0:T(8,128)}, f32[12576,768]{1,0:T(8,128)}, bf16[12576,768]{1,0:T(8,128)(2,1)}) custom-call(f32[8,128]{1,0:T(8,128)} %get-tuple-element.33.factor, f32[960,768]{1,0:T(8,128)} %collective-permute-done.7.refs_0_, ...), custom_call_target="tpu_custom_call", output_to_operand_aliasing={{0}: (6, {}), {1}: (7, {}), {2}: (8, {}), {3}: (9, {})} | custom-call | flops 2457600000 | bytes 36864000 | tf_op jit(solution)/shard_map/pallas_call | solution.py:667
  353.7 17.1 %shard_map.89 = (f32[12576,768]{1,0:T(8,128)}, f32[12576,768]{1,0:T(8,128)}, f32[12576,768]{1,0:T(8,128)}, bf16[12576,768]{1,0:T(8,128)(2,1)}) custom-call(f32[8,128]{1,0:T(8,128)} %get-tuple-element.33.factor, f32[960,768]{1,0:T(8,128)} %collective-permute-done.1.refs_0_, ...), custom_call_target="tpu_custom_call", output_to_operand_aliasing={{0}: (6, {}), {1}: (7, {}), {2}: (8, {}), {3}: (9, {})} | custom-call | flops 2457600000 | bytes 36864000 | tf_op jit(solution)/shard_map/pallas_call | solution.py:667
  370.8 0.0 collective-permute-done.5.refs_1_
  370.8 0.0 collective-permute-done.2.refs_0_
  370.8 17.1 %shard_map.90 = (f32[12576,768]{1,0:T(8,128)}, f32[12576,768]{1,0:T(8,128)}, f32[12576,768]{1,0:T(8,128)}, bf16[12576,768]{1,0:T(8,128)(2,1)}) custom-call(f32[8,128]{1,0:T(8,128)} %get-tuple-element.33.factor, f32[960,768]{1,0:T(8,128)} %collective-permute-done.2.refs_0_, ...), custom_call_target="tpu_custom_call", output_to_operand_aliasing={{0}: (6, {}), {1}: (7, {}), {2}: (8, {}), {3}: (9, {})} | custom-call | flops 2457600000 | bytes 36864000 | tf_op jit(solution)/shard_map/pallas_call | solution.py:667
Async XLA Ops:
  153.9 34.6 %collective-permute-start = (f32[960,768]{1,0:T(8,128)}, f32[960,768]{1,0:T(8,128)S(1)}, u32[]{:S(2)}, u32[]{:S(2)}) collective-permute-start(f32[960,768]{1,0:T(8,128)} %get-tuple-element.34.refs_0_), channel_id=1, source_target_pairs={{0,8},{1,25},{2,10},{3,27},{4,12},{5,29},{6,14},{7,31},{8,16},{9,1... | collective-permute-start | bytes 8847368 | tf_op jit(solution)/shard_map/ppermute | solution.py:712
  155.2 38.9 %collective-permute-start.3 = (f32[640,768]{1,0:T(8,128)}, f32[640,768]{1,0:T(8,128)S(1)}, u32[]{:S(2)}, u32[]{:S(2)}) collective-permute-start(f32[640,768]{1,0:T(8,128)} %get-tuple-element.35.refs_1_), channel_id=1, source_target_pairs={{0,2},{1,7},{2,4},{3,1},{4,6},{5,3},{6,0},{7,5},{8,10},{9,15},{10,... | collective-permute-start | bytes 5898248 | tf_op jit(solution)/shard_map/ppermute | solution.py:712
  158.6 61.6 %collective-permute-start.6 = (f32[960,768]{1,0:T(8,128)}, f32[960,768]{1,0:T(8,128)}, u32[]{:S(2)}, u32[]{:S(2)}) collective-permute-start(f32[960,768]{1,0:T(8,128)} %get-tuple-element.36.refs_2_), channel_id=1, source_target_pairs={{0,8},{1,25},{2,10},{3,27},{4,12},{5,29},{6,14},{7,31},{8,16},{9,1... | collective-permute-start | bytes 8847368 | tf_op jit(solution)/shard_map/ppermute | solution.py:712
  188.5 63.3 %collective-permute-start.1 = (f32[960,768]{1,0:T(8,128)S(1)}, f32[960,768]{1,0:T(8,128)}, u32[]{:S(2)}, u32[]{:S(2)}) collective-permute-start(f32[960,768]{1,0:T(8,128)S(1)} %collective-permute-done.refs_0_), channel_id=1, source_target_pairs={{0,8},{1,25},{2,10},{3,27},{4,12},{5,29},{6,14},{7,31},{8,16},{9,1... | collective-permute-start | bytes 8847368 | tf_op jit(solution)/shard_map/ppermute | solution.py:712
  190.6 25.3 %collective-permute-start.8 = (f32[640,768]{1,0:T(8,128)}, f32[640,768]{1,0:T(8,128)}, u32[]{:S(2)}, u32[]{:S(2)}) collective-permute-start(f32[640,768]{1,0:T(8,128)} %get-tuple-element.37.refs_3_), channel_id=1, source_target_pairs={{0,2},{1,7},{2,4},{3,1},{4,6},{5,3},{6,0},{7,5},{8,10},{9,15},{10,... | collective-permute-start | bytes 5898248 | tf_op jit(solution)/shard_map/ppermute | solution.py:712
  194.0 60.8 %collective-permute-start.11 = (f32[640,768]{1,0:T(8,128)S(1)}, f32[640,768]{1,0:T(8,128)S(1)}, u32[]{:S(2)}, u32[]{:S(2)}) collective-permute-start(f32[640,768]{1,0:T(8,128)S(1)} %collective-permute-done.3.refs_1_), channel_id=1, source_target_pairs={{0,1},{1,0},{2,3},{3,2},{4,5},{5,4},{6,7},{7,6},{8,9},{9,8},{10,11... | collective-permute-start | bytes 5898248 | tf_op jit(solution)/shard_map/ppermute | solution.py:715
  194.0 60.9 %collective-permute-start.4 = (f32[640,768]{1,0:T(8,128)S(1)}, f32[640,768]{1,0:T(8,128)}, u32[]{:S(2)}, u32[]{:S(2)}) collective-permute-start(f32[640,768]{1,0:T(8,128)S(1)} %collective-permute-done.3.refs_1_), channel_id=1, source_target_pairs={{0,2},{1,7},{2,4},{3,1},{4,6},{5,3},{6,0},{7,5},{8,10},{9,15},{10,... | collective-permute-start | bytes 5898248 | tf_op jit(solution)/shard_map/ppermute | solution.py:712
  215.9 87.7 %collective-permute-start.10 = (f32[960,768]{1,0:T(8,128)S(1)}, f32[960,768]{1,0:T(8,128)S(1)}, u32[]{:S(2)}, u32[]{:S(2)}) collective-permute-start(f32[960,768]{1,0:T(8,128)S(1)} %collective-permute-done.refs_0_), channel_id=1, source_target_pairs={{0,1},{1,0},{2,3},{3,2},{4,5},{5,4},{6,7},{7,6},{8,9},{9,8},{10,11... | collective-permute-start | bytes 8847368 | tf_op jit(solution)/shard_map/ppermute | solution.py:715
  220.2 116.8 %collective-permute-start.7 = (f32[960,768]{1,0:T(8,128)}, f32[960,768]{1,0:T(8,128)}, u32[]{:S(2)}, u32[]{:S(2)}) collective-permute-start(f32[960,768]{1,0:T(8,128)} %collective-permute-done.6.refs_0_), channel_id=1, source_target_pairs={{0,1},{1,0},{2,3},{3,2},{4,5},{5,4},{6,7},{7,6},{8,9},{9,8},{10,11... | collective-permute-start | bytes 8847368 | tf_op jit(solution)/shard_map/ppermute | solution.py:715
  251.8 119.0 %collective-permute-start.2 = (f32[960,768]{1,0:T(8,128)}, f32[960,768]{1,0:T(8,128)}, u32[]{:S(2)}, u32[]{:S(2)}) collective-permute-start(f32[960,768]{1,0:T(8,128)} %collective-permute-done.1.refs_0_), channel_id=1, source_target_pairs={{0,1},{1,0},{2,3},{3,2},{4,5},{5,4},{6,7},{7,6},{8,9},{9,8},{10,11... | collective-permute-start | bytes 8847368 | tf_op jit(solution)/shard_map/ppermute | solution.py:715
  254.9 82.1 %collective-permute-start.9 = (f32[640,768]{1,0:T(8,128)}, f32[640,768]{1,0:T(8,128)}, u32[]{:S(2)}, u32[]{:S(2)}) collective-permute-start(f32[640,768]{1,0:T(8,128)} %collective-permute-done.8.refs_1_), channel_id=1, source_target_pairs={{0,1},{1,0},{2,3},{3,2},{4,5},{5,4},{6,7},{7,6},{8,9},{9,8},{10,11... | collective-permute-start | bytes 5898248 | tf_op jit(solution)/shard_map/ppermute | solution.py:715
  254.9 115.9 %collective-permute-start.5 = (f32[640,768]{1,0:T(8,128)}, f32[640,768]{1,0:T(8,128)}, u32[]{:S(2)}, u32[]{:S(2)}) collective-permute-start(f32[640,768]{1,0:T(8,128)} %collective-permute-done.4.refs_1_), channel_id=1, source_target_pairs={{0,1},{1,0},{2,3},{3,2},{4,5},{5,4},{6,7},{7,6},{8,9},{9,8},{10,11... | collective-permute-start | bytes 5898248 | tf_op jit(solution)/shard_map/ppermute | solution.py:715
